TPU v7x, 256 devices: a whole 4x4x8 slice. The times are simulated.
256 devices in a mesh: batch: 8 (over x, core), seq: 32 (over y, z).
Axes of the slice: x: 4, y: 4, z: 8, core: 2. Of those that a mesh axis runs over, the one named last changes fastest.
Arguments:
- cotangent: bfloat16 [8, 4096, 4096], P('batch', 'seq'), may hold values from -23 to 23
- fixed_point: bfloat16 [8, 4096, 4096], P('batch', 'seq'), may hold values from -6 to 6
- input_map: bfloat16 [8, 4096, 128], P('batch', 'seq'), may hold values from -0.00390625 to 0.00390625
- output_map: bfloat16 [8, 4096, 128], P('batch', 'seq'), may hold values from -6 to 6
- step_size: float32 [8, 64, 4096], P('batch', None, 'seq'), may hold values from 0.3 to 3.4
- forget: float32 [8, 4096], P('batch', 'seq'), may hold values from 0 to 1, as said below
- decay_rate: float32 [64], replicated, may hold values from 4.8828125e-06 to 0.04
- skip_gain: float32 [64], replicated, may hold values from 0.3 to 0.65
Outputs:
- adjoint_sum: bfloat16 [8, 4096, 4096], P('batch', 'seq')
- rate_grad: float32 [64], replicated
- skip_grad: float32 [64], replicated
Inputs may be any that keep to these rules, and one draw needn't show every extreme that they name: `forget`: nonzero at few positions.
All inputs are finite; a program needn't handle non-finite values.
Results may differ from a plain program's by a relative error of at most 0.034.
Values may be sent and summed in bfloat16 or wider, within the bound.
No kernel may reach another device: no remote copies, remote signals or barrier semaphores. Data moves between devices by JAX's collectives and lax.ppermute only.
A program may use at most 128 MiB of HBM per device.

v0:
```python
import jax
import jax.numpy as jnp
from jax import lax
from jax.sharding import Mesh
from jax.sharding import PartitionSpec as P

H = 64
P_SIZE = 64
N = 128
TERMS = 4
SEQ = ("seq_0", "seq_1")
BATCH_SEQ = ("batch_0", "batch_1", "seq_0", "seq_1")
BATCH = ("batch_0", "batch_1")


def side_by_side(arrays, axis, split_dim, concat_dim, along):
    widths = [a.shape[along] for a in arrays]
    both = jnp.concatenate(arrays, axis=along)
    filled = lax.all_to_all(both, axis, split_axis=split_dim, concat_axis=concat_dim, tiled=True)
    return tuple(jnp.split(filled, [sum(widths[:k]) for k in range(1, len(widths))], axis=along))


def from_everyone(shard, axis):
    copies = jnp.broadcast_to(shard, (lax.axis_size(axis), *shard.shape))
    return lax.all_to_all(copies, axis, split_axis=0, concat_axis=0, tiled=True)


def in_order(tiles, dim):
    shape = list(tiles.shape[1:])
    shape[dim] *= tiles.shape[0]
    return jnp.moveaxis(tiles, 0, dim).reshape(shape)


def gathered_copies(shard, axis, dim):
    tiles = from_everyone(shard, axis)
    return in_order(tiles, dim)


def over_axes(shard, axes):
    for axis in axes:
        shard = lax.psum(shard, axis)
    return shard


def tables(input_rows, output_rows, step_rows, forget, decay_rate):
    log_step = -decay_rate[:, None, None] * step_rows - forget[None, :, :]
    log_decay = jnp.cumsum(log_step, axis=2)
    step_sum = jnp.cumsum(step_rows, axis=2)
    decay_end = log_decay[:, :, -1]
    block_len = log_decay.shape[2]
    causal = lax.broadcasted_iota(jnp.int32, (block_len, block_len), 0) >= lax.broadcasted_iota(
        jnp.int32, (block_len, block_len), 1
    )
    scores = jnp.einsum("ktn,ksn->kts", output_rows, input_rows, preferred_element_type=jnp.float32)
    log_gap = jnp.where(
        causal[None, None], log_decay[:, :, :, None] - log_decay[:, :, None, :], -jnp.inf
    )
    mixing = (scores[None] * jnp.exp(log_gap) * step_rows[:, :, None, :]).astype(jnp.bfloat16)
    input_weight = (
        (step_rows * jnp.exp(decay_end[:, :, None] - log_decay))[..., None]
        * input_rows[None].astype(jnp.float32)
    ).astype(jnp.bfloat16)
    output_weight = (jnp.exp(log_decay)[..., None] * output_rows[None].astype(jnp.float32)).astype(
        jnp.bfloat16
    )
    decay_run = jnp.cumsum(decay_end, axis=1)
    blocks = decay_end.shape[1]
    rows_at = lax.broadcasted_iota(jnp.int32, (blocks, blocks), 0)
    cols_at = lax.broadcasted_iota(jnp.int32, (blocks, blocks), 1)
    back_reach = jnp.exp(
        jnp.where(
            (cols_at > rows_at)[None],
            decay_run[:, None, :] - decay_end[:, None, :] - decay_run[:, :, None],
            -jnp.inf,
        )
    )
    fore_reach = jnp.exp(
        jnp.where(
            (cols_at < rows_at)[None],
            decay_run[:, :, None] - decay_end[:, :, None] - decay_run[:, None, :],
            -jnp.inf,
        )
    )
    return (
        mixing,
        input_weight,
        output_weight,
        decay_end,
        decay_run,
        step_sum,
        back_reach,
        fore_reach,
    )


def local_fore(group_table, fixed_groups):
    state_local = jnp.einsum(
        "hksn,kshp->hknp", group_table[1], fixed_groups, preferred_element_type=jnp.float32
    )
    state_own = jnp.einsum("hkj,hjnp->hknp", group_table[7], state_local)
    inner_part = jnp.einsum(
        "hkts,kshp->kthp", group_table[0], fixed_groups, preferred_element_type=jnp.float32
    )
    return (state_local, state_own, inner_part)


def local_back(group_table, vector):
    state_local = jnp.einsum(
        "hktn,kthp->hknp", group_table[2], vector, preferred_element_type=jnp.float32
    )
    state_own = jnp.einsum("hkj,hjnp->hknp", group_table[6], state_local)
    inner_part = jnp.einsum(
        "hkts,kthp->kshp", group_table[0], vector, preferred_element_type=jnp.float32
    )
    return (state_local, state_own, inner_part)


def finish(weight_rows, state_in, inner_part):
    return inner_part + jnp.einsum(
        "hksn,hknp->kshp",
        weight_rows,
        state_in.astype(jnp.bfloat16),
        preferred_element_type=jnp.float32,
    )


def pieces(step_sum, vector, fixed_groups, outputs, adjoint, state_out, state_in):
    vector_wide = vector.astype(jnp.float32)
    fixed_wide = fixed_groups.astype(jnp.float32)
    skip_part = jnp.sum(vector_wide * fixed_wide, axis=(0, 1, 3))
    step_rows = jnp.transpose(step_sum, (1, 2, 0))[..., None]
    inner_sum = jnp.sum(step_rows * (vector_wide * outputs - fixed_wide * adjoint), axis=(0, 1, 3))
    third_sum = jnp.sum(step_sum[:, :, -1][:, :, None, None] * state_out * state_in, axis=(1, 2, 3))
    return (-(inner_sum + third_sum), skip_part)


def body(cotangent, fixed_point, input_map, output_map, step_size, forget, decay_rate, skip_gain):
    sequences = cotangent.shape[0]
    length_dev = cotangent.shape[1]
    seq_count = lax.axis_size(SEQ)
    cot_rows, fixed_rows = side_by_side((cotangent, fixed_point), SEQ, 2, 1, 0)
    step_rows = lax.all_to_all(
        step_size.astype(jnp.bfloat16), SEQ, split_axis=1, concat_axis=2, tiled=True
    ).astype(step_size.dtype)
    input_rows, output_rows, forget_rows = (
        gathered_copies(input_map, SEQ, 1),
        gathered_copies(output_map, SEQ, 1),
        gathered_copies(forget.astype(jnp.bfloat16), SEQ, 1).astype(forget.dtype),
    )
    head_share = H // seq_count
    first_head = lax.axis_index(SEQ) * head_share
    own_rate = lax.dynamic_slice_in_dim(decay_rate, first_head, head_share)
    own_skip = lax.dynamic_slice_in_dim(skip_gain, first_head, head_share)
    group_shape = (sequences, seq_count, length_dev, head_share, P_SIZE)
    vector = cot_rows.reshape(group_shape)
    fixed_groups = fixed_rows.reshape(group_shape)
    group_table = jax.vmap(tables, in_axes=(0, 0, 0, 0, None))(
        input_rows.reshape(sequences, seq_count, length_dev, N),
        output_rows.reshape(sequences, seq_count, length_dev, N),
        step_rows.reshape(sequences, head_share, seq_count, length_dev),
        forget_rows.reshape(sequences, seq_count, length_dev),
        own_rate,
    )
    decay_end = group_table[3]
    state_local, state_own, inner_part = jax.vmap(local_fore)(group_table, fixed_groups)
    state_in = state_own
    outputs = jax.vmap(finish)(group_table[2], state_in, inner_part)
    state_out = state_local + jnp.exp(decay_end)[..., None, None] * state_in
    summed = jnp.zeros(group_shape, jnp.float32)
    rate_sum = jnp.zeros((H,), jnp.float32)
    skip_sum = jnp.zeros((H,), jnp.float32)
    for number in range(TERMS):
        state_local, state_own, inner_part = jax.vmap(local_back)(group_table, vector)
        state_in = state_own
        adjoint = jax.vmap(finish)(group_table[1], state_in, inner_part)
        rate_part, skip_part = jax.vmap(pieces)(
            group_table[5], vector, fixed_groups, outputs, adjoint, state_out, state_in
        )
        rate_part = lax.dynamic_update_slice_in_dim(
            jnp.zeros((H,), jnp.float32), jnp.sum(rate_part, axis=0), first_head, 0
        )
        skip_part = lax.dynamic_update_slice_in_dim(
            jnp.zeros((H,), jnp.float32), jnp.sum(skip_part, axis=0), first_head, 0
        )
        rate_part, skip_part = (over_axes(rate_part, BATCH_SEQ), over_axes(skip_part, BATCH_SEQ))
        rate_sum = rate_sum + rate_part
        skip_sum = skip_sum + skip_part
        vector_wide = vector.astype(jnp.float32)
        summed = summed + vector_wide
        if number + 1 < TERMS:
            vector = (adjoint + own_skip[None, None, None, :, None] * vector_wide).astype(
                jnp.bfloat16
            )
    result_rows = summed.astype(jnp.bfloat16).reshape(
        sequences, seq_count * length_dev, head_share * P_SIZE
    )
    result_rows = lax.all_to_all(result_rows, SEQ, split_axis=1, concat_axis=2, tiled=True)
    divisor = jnp.float32(sequences * lax.axis_size(BATCH) * length_dev * seq_count)
    return (result_rows, rate_sum / divisor, skip_sum / divisor)


def solution(mesh):
    torus = Mesh(mesh.devices.reshape(4, 2, 4, 8), ("batch_0", "batch_1", "seq_0", "seq_1"))
    return jax.shard_map(
        body,
        mesh=torus,
        in_specs=(
            P(BATCH, SEQ, None),
            P(BATCH, SEQ, None),
            P(BATCH, SEQ, None),
            P(BATCH, SEQ, None),
            P(BATCH, None, SEQ),
            P(BATCH, SEQ),
            P(),
            P(),
        ),
        out_specs=(P(BATCH, SEQ, None), P(), P()),
        check_vma=False,
    )
```

profile of v0, /device:TPU:32, one launch (start us, length us, event | category | flops | bytes accessed | tf_op | source)
XLA Modules:
  0.0 298.1 jit_solution(10278016321710463408)
XLA Ops:
  1.9 11.4 %all-to-all-start.4 = ((bf16[32,1,128]{2,1,0:T(2,128)(2,1)}), bf16[32,1,128]{2,1,0:T(2,128)(2,1)S(1)}, u32[]{:S(2)}, u32[]{:S(2)}) async-start(bf16[32,1,128]{2,1,0:T(2,128)(2,1)} %broadcast_in_dim.68), calls=%async_computation.4 | async-start | bytes 32768 | tf_op jit(solution)/shard_map/all_to_all | solution.py:25
  14.1 7.8 %all-to-all-done.4 = bf16[32,1,128]{2,1,0:T(2,128)(2,1)S(1)} async-done(((bf16[32,1,128]{2,1,0:T(2,128)(2,1)}), bf16[32,1,128]{2,1,0:T(2,128)(2,1)S(1)}, u32[]{:S(2)}, u32[]{:S(2)}) %all-to-all-start.4) | async-done | bytes 8224 | tf_op jit(solution)/shard_map/all_to_all | solution.py:25
  21.9 12.8 %all_to_all.57 = bf16[32,2,128]{2,1,0:T(2,128)(2,1)S(1)} all-to-all(bf16[32,2,128]{2,1,0:T(2,128)(2,1)S(1)} %bitcast.176), channel_id=1, replica_groups=mesh['batch_0'=4,'batch_1'=2,'seq_0'=4,'seq_1'=8] {'seq_0','seq_1'}, dimensions={0} | all-to-all | bytes 32768 | tf_op jit(solution)/shard_map/all_to_all | solution.py:142
  35.6 30.5 %all_to_all.58 = bf16[32,1,128,128]{3,2,1,0:T(8,128)(2,1)S(1)} all-to-all(bf16[32,1,128,128]{3,2,1,0:T(8,128)(2,1)S(1)} %broadcast_in_dim.40), channel_id=1, replica_groups=mesh['batch_0'=4,'batch_1'=2,'seq_0'=4,'seq_1'=8] {'seq_0','seq_1'}, dimensions={0} | all-to-all | bytes 2097152 | tf_op jit(solution)/shard_map/all_to_all | solution.py:25
  67.4 5.1 %all-to-all-start.2 = ((bf16[32,1,128,128]{3,2,1,0:T(8,128)(2,1)}), bf16[32,1,128,128]{3,2,1,0:T(8,128)(2,1)S(1)}, u32[]{:S(2)}, u32[]{:S(2)}) async-start(bf16[32,1,128,128]{3,2,1,0:T(8,128)(2,1)} %broadcast_in_dim.66), calls=%async_computation.2 | async-start | bytes 2097152 | tf_op jit(solution)/shard_map/all_to_all | solution.py:25
  72.5 2.8 pad_maximum_fusion
  75.2 6.2 %copy.112 = bf16[2,128,4096]{1,0,2:T(2,128)(2,1)} copy(bf16[2,128,4096]{2,1,0:T(8,128)(2,1)} %pad_maximum_fusion) | data formatting | bytes 4194304 | tf_op jit(solution)/shard_map/concatenate | solution.py:18
  81.4 16.6 %all-to-all-done.2 = bf16[32,1,128,128]{3,2,1,0:T(8,128)(2,1)S(1)} async-done(((bf16[32,1,128,128]{3,2,1,0:T(8,128)(2,1)}), bf16[32,1,128,128]{3,2,1,0:T(8,128)(2,1)S(1)}, u32[]{:S(2)}, u32[]{:S(2)}) %all-to-all-start.2) | async-done | bytes 1048608 | tf_op jit(solution)/shard_map/all_to_all | solution.py:25
  98.0 5.2 %all-to-all-start = ((bf16[2,128,4096]{1,0,2:T(2,128)(2,1)}), bf16[2,128,4096]{1,0,2:T(2,128)(2,1)}, u32[]{:S(2)}, u32[]{:S(2)}) async-start(bf16[2,128,4096]{1,0,2:T(2,128)(2,1)} %copy.112), calls=%async_computation | async-start | bytes 4194304 | tf_op jit(solution)/shard_map/all_to_all | solution.py:19
  111.2 38.6 %all-to-all-done = bf16[2,128,4096]{1,0,2:T(2,128)(2,1)} async-done(((bf16[2,128,4096]{1,0,2:T(2,128)(2,1)}), bf16[2,128,4096]{1,0,2:T(2,128)(2,1)}, u32[]{:S(2)}, u32[]{:S(2)}) %all-to-all-start) | async-done | bytes 2097184 | tf_op jit(solution)/shard_map/all_to_all | solution.py:19
  177.5 4.0 %add_multiply_fusion = (f32[2,32,128,64]{2,1,3,0:T(8,128)}, bf16[2,32,128,64]{2,1,3,0:T(8,128)(2,1)S(1)}) fusion(f32[2,32,128,64]{2,3,1,0:T(8,128)S(1)} %fusion.33, f32[2,32]{1,0:T(2,128)S(1)} %get-tuple-element.40, f32[2,32]{1,0:T(2,128)S(1)} %slice_reduce_fusion, f32[2,32]{1,0:T(2,128)S(1)} %bitcast.173, f32[2,32]{1,0:T(2,128)S(1)} %subtract_reduce_fusion, ...), kind=kOutput, calls=%fused_computation.68 | convolution fusion | flops 35655680 | bytes 5244928 | tf_op jit(solution)/shard_map/vmap(hkj,hjnp->hknp)/dot_general | solution.py:100
  181.4 3.0 %fusion.59 = f32[32,2,64,128]{3,2,1,0:T(8,128)S(1)} fusion(f32[32,2,64,128]{3,2,1,0:T(8,128)S(1)} %fusion.116, bf16[2,32,128,64]{2,1,3,0:T(8,128)(2,1)S(1)} %get-tuple-element.33, f32[32,128,128]{2,1,0:T(8,128)S(1)} %copy-done, f32[2,32,128]{2,1,0:T(8,128)S(1)} %bitcast_exponential_fusion), kind=kOutput, calls=%fused_computation.87 | convolution fusion | flops 136839168 | bytes 7372800 | tf_op jit(solution)/shard_map/vmap(hksn,hknp->kshp)/dot_general | solution.py:119
  184.5 4.1 %fusion.23 = (f32[2]{0:T(128)S(1)}, f32[2]{0:T(128)S(1)}, f32[2]{0:T(128)S(1)}, f32[2]{0:T(128)S(1)}, f32[2]{0:T(128)S(1)}, /*index=5*/f32[2]{0:T(128)S(1)}, bf16[1,32,128,2,64]{2,4,3,1,0:T(8,128)(2,1)S(1)}) fusion(bf16[1,32,128,2,64]{2,4,3,1,0:T(8,128)(2,1)S(1)} %get-tuple-element.48, f32[1,32,128,2,64]{2,4,3,1,0:T(8,128)S(1)} %bitcast.151, ...), kind=kOutput, calls=%fused_computation.37 | convolution fusion | flops 150994944 | bytes 18939960 | tf_op jit(solution)/shard_map/vmap(hksn,hknp->kshp)/dot_general | solution.py:119
  188.6 2.5 fusion.3
  193.0 5.5 %copy.147 = bf16[1,32,128,2,64]{4,3,2,1,0:T(2,128)(2,1)} copy(bf16[1,32,128,2,64]{2,4,3,1,0:T(8,128)(2,1)} %fusion.8) | data formatting | bytes 2097152 | tf_op jit(solution)/shard_map/reshape | solution.py:194
  198.5 8.7 %reshape.401 = bf16[1,4096,128]{2,0,1:T(2,128)(2,1)} reshape(bf16[1,32,128,2,64]{4,3,2,1,0:T(2,128)(2,1)} %copy.147) | data formatting | bytes 2097152 | tf_op jit(solution)/shard_map/reshape | solution.py:194
  207.8 24.4 %reduce.26 = bf16[4096,128]{1,0:T(8,128)(2,1)} reduce(bf16[4096,1,128]{2,1,0:T(2,128)(2,1)} %bitcast.154, bf16[]{:T(256)} %broadcast.176), dimensions={1}, to_apply=%bitcast.117.reduce_sub_computation | reduce | bytes 2097154
  234.3 6.1 %all-to-all-start.5 = ((bf16[32,2,8192]{2,1,0:T(2,128)(2,1)}), bf16[32,2,8192]{2,1,0:T(2,128)(2,1)}, u32[]{:S(2)}, u32[]{:S(2)}) async-start(bf16[32,2,8192]{2,1,0:T(2,128)(2,1)} %reshape.408), calls=%async_computation.5 | async-start | bytes 2097152 | tf_op jit(solution)/shard_map/all_to_all | solution.py:197
  241.0 5.4 %multiply_reduce_fusion.1 = (f32[2]{0:T(128)S(1)}, f32[2]{0:T(128)S(1)}, f32[2]{0:T(128)S(1)}, f32[2]{0:T(128)S(1)}, bf16[2,32,128,64]{2,1,3,0:T(8,128)(2,1)S(1)}) fusion(f32[2,32,128,64]{2,1,3,0:T(8,128)} %get-tuple-element.32, f32[2,32,128,64]{2,1,3,0:T(8,128)} %get-tuple-element.51, f32[2,32,128,64]{2,1,3,0:T(8,128)} %get-tuple-element.47, ...), kind=kOutput, calls=%fused_computation.64 | convolution fusion | flops 38277120 | bytes 10487328 | tf_op jit(solution)/shard_map/vmap(hkj,hjnp->hknp)/dot_general | solution.py:111
  251.7 10.5 %all-reduce.2 = (f32[64]{0:T(128)S(1)}, f32[64]{0:T(128)S(1)}) all-reduce(f32[64]{0:T(128)S(1)} %get-tuple-element.55, f32[64]{0:T(128)S(1)} %get-tuple-element.54), channel_id=1, replica_groups=mesh['batch_0'=4,'batch_1'=2,'seq_0'=4,'seq_1'=8] {'batch_0'}, use_global_device_ids=true, to_apply=%region_5.6 | all-reduce | flops 128 | bytes 1024 | tf_op jit(solution)/shard_map/psum | solution.py:41
  262.2 2.5 all-reduce.3
  264.6 10.4 %all-reduce.1 = (f32[64]{0:T(128)S(1)}, f32[64]{0:T(128)S(1)}) all-reduce(f32[64]{0:T(128)S(1)} %get-tuple-element.28, f32[64]{0:T(128)S(1)} %get-tuple-element.29), channel_id=1, replica_groups=mesh['batch_0'=4,'batch_1'=2,'seq_0'=4,'seq_1'=8] {'seq_0'}, use_global_device_ids=true, to_apply=%region_7.8 | all-reduce | flops 128 | bytes 1024 | tf_op jit(solution)/shard_map/psum | solution.py:41
  275.0 15.6 %all-reduce = (f32[64]{0:T(128)S(1)}, f32[64]{0:T(128)S(1)}) all-reduce(f32[64]{0:T(128)S(1)} %get-tuple-element.24, f32[64]{0:T(128)S(1)} %get-tuple-element.25), channel_id=1, replica_groups=mesh['batch_0'=4,'batch_1'=2,'seq_0'=4,'seq_1'=8] {'seq_1'}, use_global_device_ids=true, to_apply=%region_8.9 | all-reduce | flops 128 | bytes 1024 | tf_op jit(solution)/shard_map/psum | solution.py:41
  291.7 4.3 %reshape.409 = bf16[4096,1,128]{2,1,0:T(2,128)(2,1)S(1)} reshape(bf16[32,2,8192]{2,1,0:T(2,128)(2,1)} %all-to-all-done.5) | data formatting | bytes 2097152
  (99 shorter events, 53.2 us)
Async XLA Ops:
  0.6 65.5 %copy-start.10 = (bf16[1,128,128]{2,1,0:T(8,128)(2,1)S(1)}, bf16[1,128,128]{2,1,0:T(8,128)(2,1)}, u32[]{:S(2)}) copy-start(bf16[1,128,128]{2,1,0:T(8,128)(2,1)} %param.10) | copy-start | bytes 98308
  1.9 19.9 %all-to-all-start.4 = ((bf16[32,1,128]{2,1,0:T(2,128)(2,1)}), bf16[32,1,128]{2,1,0:T(2,128)(2,1)S(1)}, u32[]{:S(2)}, u32[]{:S(2)}) async-start(bf16[32,1,128]{2,1,0:T(2,128)(2,1)} %broadcast_in_dim.68), calls=%async_computation.4 | async-start | bytes 32768 | tf_op jit(solution)/shard_map/all_to_all | solution.py:25
  66.2 6.3 %copy-start.9 = (bf16[1,128,4096]{2,1,0:T(8,128)(2,1)S(1)}, bf16[1,128,4096]{2,1,0:T(8,128)(2,1)}, u32[]{:S(2)}) copy-start(bf16[1,128,4096]{2,1,0:T(8,128)(2,1)} %param.9) | copy-start | bytes 3145732
  67.4 30.7 %all-to-all-start.2 = ((bf16[32,1,128,128]{3,2,1,0:T(8,128)(2,1)}), bf16[32,1,128,128]{3,2,1,0:T(8,128)(2,1)S(1)}, u32[]{:S(2)}, u32[]{:S(2)}) async-start(bf16[32,1,128,128]{3,2,1,0:T(8,128)(2,1)} %broadcast_in_dim.66), calls=%async_computation.2 | async-start | bytes 2097152 | tf_op jit(solution)/shard_map/all_to_all | solution.py:25
  81.4 21.9 %copy-start.11 = (f32[64]{0:T(128)S(1)}, f32[64]{0:T(128)}, u32[]{:S(2)}) copy-start(f32[64]{0:T(128)} %param.15) | copy-start | bytes 772
  81.4 22.0 %copy-start.12 = (f32[64]{0:T(128)S(1)}, f32[64]{0:T(128)}, u32[]{:S(2)}) copy-start(f32[64]{0:T(128)} %param.14) | copy-start | bytes 772
  98.0 5.3 %copy-start.1 = (bf16[32,1,128,128]{3,2,1,0:T(8,128)(2,1)}, bf16[32,1,128,128]{3,2,1,0:T(8,128)(2,1)S(1)}, u32[]{:S(2)}) copy-start(bf16[32,1,128,128]{3,2,1,0:T(8,128)(2,1)S(1)} %all-to-all-done.2) | copy-start | bytes 3145732
  98.0 51.8 %all-to-all-start = ((bf16[2,128,4096]{1,0,2:T(2,128)(2,1)}), bf16[2,128,4096]{1,0,2:T(2,128)(2,1)}, u32[]{:S(2)}, u32[]{:S(2)}) async-start(bf16[2,128,4096]{1,0,2:T(2,128)(2,1)} %copy.112), calls=%async_computation | async-start | bytes 4194304 | tf_op jit(solution)/shard_map/all_to_all | solution.py:19
  107.5 1.6 copy-start.2
  152.0 1.6 copy-start
  152.9 31.6 %copy-start.5 = (f32[1,32,128,128]{2,3,1,0:T(8,128)}, f32[1,32,128,128]{2,3,1,0:T(8,128)S(1)}, u32[]{:S(2)}) copy-start(f32[1,32,128,128]{2,3,1,0:T(8,128)S(1)} %get-tuple-element.35) | copy-start | bytes 6291460
  155.2 2.2 copy-start.7
  184.5 4.1 %copy-start.3 = (f32[32,2,64,128]{3,2,1,0:T(8,128)}, f32[32,2,64,128]{3,2,1,0:T(8,128)S(1)}, u32[]{:S(2)}) copy-start(f32[32,2,64,128]{3,2,1,0:T(8,128)S(1)} %fusion.59) | copy-start | bytes 6291460
  234.3 57.3 %all-to-all-start.5 = ((bf16[32,2,8192]{2,1,0:T(2,128)(2,1)}), bf16[32,2,8192]{2,1,0:T(2,128)(2,1)}, u32[]{:S(2)}, u32[]{:S(2)}) async-start(bf16[32,2,8192]{2,1,0:T(2,128)(2,1)} %reshape.408), calls=%async_computation.5 | async-start | bytes 2097152 | tf_op jit(solution)/shard_map/all_to_all | solution.py:197
  241.0 8.2 %copy-start.8 = (f32[32,128,128]{2,1,0:T(8,128)S(1)}, f32[32,128,128]{2,1,0:T(8,128)}, u32[]{:S(2)}) copy-start(f32[32,128,128]{2,1,0:T(8,128)} %fusion.65) | copy-start | bytes 6291460
  246.9 2.3 copy-start.4
  246.9 2.3 copy-start.6
where the time goes:
time: 300 us; the launch traced here: 298 us
  blocking collectives  82.3 us (27%)
  waiting for transfers between devices  63 us (21%)
  matrix products  49.2 us (16%)
  other arithmetic  38.7 us (13%)
  local copies, waits for them, and re-layouts  36.1 us (12%)
  starting transfers between devices  27.8 us (9%)
    psum x4, blocking collectives, over_axes(): shard = lax.psum(shard, axis)  39 us
    all_to_all x1, waiting for transfers between devices, side_by_side(): lax.all_to_all(both, axis, split_axis=split_dim, concat_axis=concat_dim,...  38.6 us
    all_to_all x1, blocking collectives, from_everyone(): return lax.all_to_all(copies, axis, split_axis=0, concat_axis=0, tiled=True)  30.5 us
    unnamed x1, other arithmetic  24.4 us
    all_to_all x2, waiting for transfers between devices, from_everyone(): return lax.all_to_all(copies, axis, split_axis=0, concat_axis=0, tiled=True)  24.4 us
    all_to_all x2, starting transfers between devices, from_everyone(): return lax.all_to_all(copies, axis, split_axis=0, concat_axis=0, tiled=True)  16.4 us
    reshape x2, local copies, waits for them, and re-layouts, body(): summed.astype(jnp.bfloat16)  14.3 us
    dot_general x5, matrix products, finish(): jnp.einsum('hksn,hknp->kshp', weight_rows, state_in.astype(jnp.bfloat16),...  13.3 us
  transfers between devices with their start and end apart: 4, of which 3 were waited for; matrix products, arithmetic and copies ran while one was open for 10% of the time, Pallas kernels for 0%

commit v1 on v0

--- a/solution.py
+++ b/solution.py
@@ -38,7 +38,7 @@
 
 def over_axes(shard, axes):
     for axis in axes:
-        shard = lax.psum(shard, axis)
+        shard = jnp.sum(lax.all_gather(shard, axis), axis=0)
     return shard
 
 

time: 300 us -> 380 us (1.27); the launches traced: 298 us -> 373 us
  blocking collectives: 82.3 us -> 149 us
  local copies, waits for them, and re-layouts: 36.1 us -> 48.3 us
  waiting for transfers between devices: 63 us -> 59.1 us
    all_gather x0 -> x8, blocking collectives: none -> 64.6 us  [over_axes(): shard = jnp.sum(lax.all_gather(shard, axis), axis=0)]
    unnamed x0 -> x3, blocking collectives: none -> 41 us
    psum x4 -> x0, blocking collectives: 39 us -> none  [over_axes(): shard = lax.psum(shard, axis)]
    unnamed x33 -> x94, local copies, waits for them, and re-layouts: 9.12 us -> 17.7 us
    dot_general x4, matrix products: 11.9 us -> 4.81 us  [local_back(): state_own = jnp.einsum('hkj,hjnp->hknp', group_table[6], state_local)]
    all_to_all x1, waiting for transfers between devices: 38.6 us -> 34.7 us  [side_by_side(): lax.all_to_all(both, axis, split_axis=split_dim, concat_axis=concat_dim,...]
    unnamed x1 -> x5, other arithmetic: 24.4 us -> 24.4 us
where the time goes in v1:
time: 380 us; the launch traced here: 373 us
  blocking collectives  149 us (39%)
  waiting for transfers between devices  59.1 us (16%)
  local copies, waits for them, and re-layouts  48.3 us (13%)
  matrix products  46.4 us (12%)
  other arithmetic  38.5 us (10%)
  starting transfers between devices  28.5 us (8%)
    all_gather x8, blocking collectives, over_axes(): shard = jnp.sum(lax.all_gather(shard, axis), axis=0)  64.6 us
    unnamed x3, blocking collectives  41 us
    all_to_all x1, waiting for transfers between devices, side_by_side(): lax.all_to_all(both, axis, split_axis=split_dim, concat_axis=concat_dim,...  34.7 us
    all_to_all x1, blocking collectives, from_everyone(): return lax.all_to_all(copies, axis, split_axis=0, concat_axis=0, tiled=True)  30.5 us
    unnamed x5, other arithmetic  24.4 us
    all_to_all x2, waiting for transfers between devices, from_everyone(): return lax.all_to_all(copies, axis, split_axis=0, concat_axis=0, tiled=True)  24.3 us
    unnamed x94, local copies, waits for them, and re-layouts  17.7 us
    all_to_all x2, starting transfers between devices, from_everyone(): return lax.all_to_all(copies, axis, split_axis=0, concat_axis=0, tiled=True)  16.4 us
  transfers between devices with their start and end apart: 4, of which 3 were waited for; matrix products, arithmetic and copies ran while one was open for 10% of the time, Pallas kernels for 0%

profile of v1, /device:TPU:32, one launch (start us, length us, event | category | flops | bytes accessed | tf_op | source)
XLA Modules:
  0.0 373.0 jit_solution(3782296019550796253)
XLA Ops:
  1.9 11.4 %all-to-all-start.4 = ((bf16[32,1,128]{2,1,0:T(2,128)(2,1)}), bf16[32,1,128]{2,1,0:T(2,128)(2,1)S(1)}, u32[]{:S(2)}, u32[]{:S(2)}) async-start(bf16[32,1,128]{2,1,0:T(2,128)(2,1)} %broadcast_in_dim.68), calls=%async_computation.4 | async-start | bytes 32768 | tf_op jit(solution)/shard_map/all_to_all | solution.py:25
  14.1 7.8 %all-to-all-done.4 = bf16[32,1,128]{2,1,0:T(2,128)(2,1)S(1)} async-done(((bf16[32,1,128]{2,1,0:T(2,128)(2,1)}), bf16[32,1,128]{2,1,0:T(2,128)(2,1)S(1)}, u32[]{:S(2)}, u32[]{:S(2)}) %all-to-all-start.4) | async-done | bytes 8224 | tf_op jit(solution)/shard_map/all_to_all | solution.py:25
  21.9 12.8 %all_to_all.57 = bf16[32,2,128]{2,1,0:T(2,128)(2,1)S(1)} all-to-all(bf16[32,2,128]{2,1,0:T(2,128)(2,1)S(1)} %bitcast.191), channel_id=1, replica_groups=mesh['batch_0'=4,'batch_1'=2,'seq_0'=4,'seq_1'=8] {'seq_0','seq_1'}, dimensions={0} | all-to-all | bytes 32768 | tf_op jit(solution)/shard_map/all_to_all | solution.py:142
  35.6 30.5 %all_to_all.58 = bf16[32,1,128,128]{3,2,1,0:T(8,128)(2,1)S(1)} all-to-all(bf16[32,1,128,128]{3,2,1,0:T(8,128)(2,1)S(1)} %broadcast_in_dim.40), channel_id=1, replica_groups=mesh['batch_0'=4,'batch_1'=2,'seq_0'=4,'seq_1'=8] {'seq_0','seq_1'}, dimensions={0} | all-to-all | bytes 2097152 | tf_op jit(solution)/shard_map/all_to_all | solution.py:25
  67.4 5.1 %all-to-all-start.2 = ((bf16[32,1,128,128]{3,2,1,0:T(8,128)(2,1)}), bf16[32,1,128,128]{3,2,1,0:T(8,128)(2,1)S(1)}, u32[]{:S(2)}, u32[]{:S(2)}) async-start(bf16[32,1,128,128]{3,2,1,0:T(8,128)(2,1)} %broadcast_in_dim.66), calls=%async_computation.2 | async-start | bytes 2097152 | tf_op jit(solution)/shard_map/all_to_all | solution.py:25
  75.2 6.2 %copy.145 = bf16[2,128,4096]{1,0,2:T(2,128)(2,1)} copy(bf16[2,128,4096]{2,1,0:T(8,128)(2,1)} %pad_maximum_fusion) | data formatting | bytes 4194304 | tf_op jit(solution)/shard_map/concatenate | solution.py:18
  81.4 16.6 %all-to-all-done.2 = bf16[32,1,128,128]{3,2,1,0:T(8,128)(2,1)S(1)} async-done(((bf16[32,1,128,128]{3,2,1,0:T(8,128)(2,1)}), bf16[32,1,128,128]{3,2,1,0:T(8,128)(2,1)S(1)}, u32[]{:S(2)}, u32[]{:S(2)}) %all-to-all-start.2) | async-done | bytes 1048608 | tf_op jit(solution)/shard_map/all_to_all | solution.py:25
  98.0 5.9 %all-to-all-start = ((bf16[2,128,4096]{1,0,2:T(2,128)(2,1)}), bf16[2,128,4096]{1,0,2:T(2,128)(2,1)}, u32[]{:S(2)}, u32[]{:S(2)}) async-start(bf16[2,128,4096]{1,0,2:T(2,128)(2,1)} %copy.145), calls=%async_computation | async-start | bytes 4194304 | tf_op jit(solution)/shard_map/all_to_all | solution.py:19
  115.6 34.7 %all-to-all-done = bf16[2,128,4096]{1,0,2:T(2,128)(2,1)} async-done(((bf16[2,128,4096]{1,0,2:T(2,128)(2,1)}), bf16[2,128,4096]{1,0,2:T(2,128)(2,1)}, u32[]{:S(2)}, u32[]{:S(2)}) %all-to-all-start) | async-done | bytes 2097184 | tf_op jit(solution)/shard_map/all_to_all | solution.py:19
  182.3 5.6 %fusion.17 = (f32[2]{0:T(128)S(1)}, f32[2]{0:T(128)S(1)}, f32[2]{0:T(128)S(1)}, f32[2]{0:T(128)S(1)}, f32[2]{0:T(128)S(1)}, /*index=5*/f32[2]{0:T(128)S(1)}, bf1...) fusion(bf16[1,32,128,2,64]{2,4,3,1,0:T(8,128)(2,1)S(1)} %get-tuple-element.63, ...), kind=kOutput, calls=%fused_computation.31 | convolution fusion | flops 150994944 | bytes 21037112 | tf_op jit(solution)/shard_map/vmap(hksn,hknp->kshp)/dot_general | solution.py:119
  194.0 9.7 %all-gather.25 = f32[4,1,64]{2,1,0:T(1,128)S(1)} all-gather(f32[1,1,64]{2,1,0:T(1,128)S(1)} %dynamic_update_slice.41), channel_id=1, replica_groups=mesh['batch_0'=4,'batch_1'=2,'seq_0'=4,'seq_1'=8] {'batch_0'}, dimensions={0}, use_global_device_ids=true | all-gather | bytes 1280 | tf_op jit(solution)/shard_map/all_gather | solution.py:41
  203.8 5.7 %copy.180 = bf16[1,32,128,2,64]{4,3,2,1,0:T(2,128)(2,1)} copy(bf16[1,32,128,2,64]{2,4,3,1,0:T(8,128)(2,1)} %fusion.8) | data formatting | bytes 2097152 | tf_op jit(solution)/shard_map/reshape | solution.py:194
  209.6 8.7 %reshape.653 = bf16[1,4096,128]{2,0,1:T(2,128)(2,1)} reshape(bf16[1,32,128,2,64]{4,3,2,1,0:T(2,128)(2,1)} %copy.180) | data formatting | bytes 2097152 | tf_op jit(solution)/shard_map/reshape | solution.py:194
  218.8 24.4 %reduce.34 = bf16[4096,128]{1,0:T(8,128)(2,1)} reduce(bf16[4096,1,128]{2,1,0:T(2,128)(2,1)} %bitcast.169, bf16[]{:T(256)} %broadcast.214), dimensions={1}, to_apply=%bitcast.132.reduce_sub_computation | reduce | bytes 2097154
  245.4 6.1 %all-to-all-start.5 = ((bf16[32,2,8192]{2,1,0:T(2,128)(2,1)}), bf16[32,2,8192]{2,1,0:T(2,128)(2,1)}, u32[]{:S(2)}, u32[]{:S(2)}) async-start(bf16[32,2,8192]{2,1,0:T(2,128)(2,1)} %reshape.660), calls=%async_computation.5 | async-start | bytes 2097152 | tf_op jit(solution)/shard_map/all_to_all | solution.py:197
  251.8 7.0 %all-gather.24 = f32[4,1,64]{2,1,0:T(1,128)S(1)} all-gather(f32[1,1,64]{2,1,0:T(1,128)S(1)} %dynamic_update_slice.40), channel_id=1, replica_groups=mesh['batch_0'=4,'batch_1'=2,'seq_0'=4,'seq_1'=8] {'batch_0'}, dimensions={0}, use_global_device_ids=true | all-gather | bytes 1280 | tf_op jit(solution)/shard_map/all_gather | solution.py:41
  259.5 9.0 %all-gather.26 = f32[4,1,64]{2,1,0:T(1,128)S(1)} all-gather(f32[1,1,64]{2,1,0:T(1,128)S(1)} %dynamic_update_slice.42), channel_id=1, replica_groups=mesh['batch_0'=4,'batch_1'=2,'seq_0'=4,'seq_1'=8] {'batch_0'}, dimensions={0}, use_global_device_ids=true | all-gather | bytes 1280 | tf_op jit(solution)/shard_map/all_gather | solution.py:41
  276.6 7.0 %all-gather.27 = f32[4,1,64]{2,1,0:T(1,128)S(1)} all-gather(f32[1,1,64]{2,1,0:T(1,128)S(1)} %dynamic_update_slice.43), channel_id=1, replica_groups=mesh['batch_0'=4,'batch_1'=2,'seq_0'=4,'seq_1'=8] {'batch_0'}, dimensions={0}, use_global_device_ids=true | all-gather | bytes 1280 | tf_op jit(solution)/shard_map/all_gather | solution.py:41
  284.0 9.0 %all-gather.29 = f32[4,1,64]{2,1,0:T(1,128)S(1)} all-gather(f32[1,1,64]{2,1,0:T(1,128)S(1)} %dynamic_update_slice.45), channel_id=1, replica_groups=mesh['batch_0'=4,'batch_1'=2,'seq_0'=4,'seq_1'=8] {'batch_0'}, dimensions={0}, use_global_device_ids=true | all-gather | bytes 1280 | tf_op jit(solution)/shard_map/all_gather | solution.py:41
  293.5 7.0 %all-gather.30 = f32[4,1,64]{2,1,0:T(1,128)S(1)} all-gather(f32[1,1,64]{2,1,0:T(1,128)S(1)} %dynamic_update_slice.46), channel_id=1, replica_groups=mesh['batch_0'=4,'batch_1'=2,'seq_0'=4,'seq_1'=8] {'batch_0'}, dimensions={0}, use_global_device_ids=true | all-gather | bytes 1280 | tf_op jit(solution)/shard_map/all_gather | solution.py:41
  300.9 9.0 %all-gather.31 = f32[4,1,64]{2,1,0:T(1,128)S(1)} all-gather(f32[1,1,64]{2,1,0:T(1,128)S(1)} %dynamic_update_slice.47), channel_id=1, replica_groups=mesh['batch_0'=4,'batch_1'=2,'seq_0'=4,'seq_1'=8] {'batch_0'}, dimensions={0}, use_global_device_ids=true | all-gather | bytes 1280 | tf_op jit(solution)/shard_map/all_gather | solution.py:41
  310.5 7.0 %all-gather.28 = f32[4,1,64]{2,1,0:T(1,128)S(1)} all-gather(f32[1,1,64]{2,1,0:T(1,128)S(1)} %dynamic_update_slice.44), channel_id=1, replica_groups=mesh['batch_0'=4,'batch_1'=2,'seq_0'=4,'seq_1'=8] {'batch_0'}, dimensions={0}, use_global_device_ids=true | all-gather | bytes 1280 | tf_op jit(solution)/shard_map/all_gather | solution.py:41
  323.2 10.5 %all-reduce.25 = (f32[256]{0:T(256)S(1)}, f32[256]{0:T(256)S(1)}, f32[256]{0:T(256)S(1)}, f32[256]{0:T(256)S(1)}, f32[256]{0:T(256)S(1)}, /*index=5*/f32[256]{0:T(256)S(1)}, f32[256]{0:T(256)S(1)}, f32[256]{0:T(256)S(1)}) all-reduce(f32[256]{0:T(256)S(1)} %dynamic-update-slice.10, ...), channel_id=12, replica_groups=mesh['batch_0'=4,'batch_1'=2,'seq_0'=4,'seq_1'=8] {'seq_0'}, use_global_device_ids=true, to_apply=%add.10 | all-reduce | flops 2048 | bytes 16384
  336.5 28.1 %all-reduce.24 = (f32[512]{0:T(512)S(1)}, f32[512]{0:T(512)S(1)}, f32[512]{0:T(512)S(1)}, f32[512]{0:T(512)S(1)}, f32[512]{0:T(512)S(1)}, /*index=5*/f32[512]{0:T(512)S(1)}, f32[512]{0:T(512)S(1)}, f32[512]{0:T(512)S(1)}) all-reduce(f32[512]{0:T(512)S(1)} %dynamic-update-slice.11, ...), channel_id=13, replica_groups=mesh['batch_0'=4,'batch_1'=2,'seq_0'=4,'seq_1'=8] {'seq_1'}, use_global_device_ids=true, to_apply=%add.11 | all-reduce | flops 4096 | bytes 32768
  (225 shorter events, 85.0 us)
Async XLA Ops:
  0.6 65.5 %copy-start.8 = (bf16[1,128,128]{2,1,0:T(8,128)(2,1)S(1)}, bf16[1,128,128]{2,1,0:T(8,128)(2,1)}, u32[]{:S(2)}) copy-start(bf16[1,128,128]{2,1,0:T(8,128)(2,1)} %param.10) | copy-start | bytes 98308
  1.9 19.9 %all-to-all-start.4 = ((bf16[32,1,128]{2,1,0:T(2,128)(2,1)}), bf16[32,1,128]{2,1,0:T(2,128)(2,1)S(1)}, u32[]{:S(2)}, u32[]{:S(2)}) async-start(bf16[32,1,128]{2,1,0:T(2,128)(2,1)} %broadcast_in_dim.68), calls=%async_computation.4 | async-start | bytes 32768 | tf_op jit(solution)/shard_map/all_to_all | solution.py:25
  66.2 6.3 %copy-start.7 = (bf16[1,128,4096]{2,1,0:T(8,128)(2,1)S(1)}, bf16[1,128,4096]{2,1,0:T(8,128)(2,1)}, u32[]{:S(2)}) copy-start(bf16[1,128,4096]{2,1,0:T(8,128)(2,1)} %param.9) | copy-start | bytes 3145732
  67.4 30.7 %all-to-all-start.2 = ((bf16[32,1,128,128]{3,2,1,0:T(8,128)(2,1)}), bf16[32,1,128,128]{3,2,1,0:T(8,128)(2,1)S(1)}, u32[]{:S(2)}, u32[]{:S(2)}) async-start(bf16[32,1,128,128]{3,2,1,0:T(8,128)(2,1)} %broadcast_in_dim.66), calls=%async_computation.2 | async-start | bytes 2097152 | tf_op jit(solution)/shard_map/all_to_all | solution.py:25
  81.4 22.6 %copy-start.13 = (u32[256]{0:T(256)S(1)}, u32[256]{0:T(256)}, u32[]{:S(2)}) copy-start(u32[256]{0:T(256)} %constant.48) | copy-start | bytes 3076
  81.4 23.2 %copy-start.12 = (u32[256]{0:T(256)S(1)}, u32[256]{0:T(256)}, u32[]{:S(2)}) copy-start(u32[256]{0:T(256)} %constant.53) | copy-start | bytes 3076
  81.4 25.1 %copy-start.11 = (u32[256]{0:T(256)S(1)}, u32[256]{0:T(256)}, u32[]{:S(2)}) copy-start(u32[256]{0:T(256)} %constant.58) | copy-start | bytes 3076
  81.4 26.4 %copy-start.9 = (f32[64]{0:T(128)S(1)}, f32[64]{0:T(128)}, u32[]{:S(2)}) copy-start(f32[64]{0:T(128)} %param.15) | copy-start | bytes 772
  81.4 26.5 %copy-start.10 = (f32[64]{0:T(128)S(1)}, f32[64]{0:T(128)}, u32[]{:S(2)}) copy-start(f32[64]{0:T(128)} %param.14) | copy-start | bytes 772
  98.0 6.0 %copy-start.1 = (bf16[32,1,128,128]{3,2,1,0:T(8,128)(2,1)}, bf16[32,1,128,128]{3,2,1,0:T(8,128)(2,1)S(1)}, u32[]{:S(2)}) copy-start(bf16[32,1,128,128]{3,2,1,0:T(8,128)(2,1)S(1)} %all-to-all-done.2) | copy-start | bytes 3145732
  98.0 52.3 %all-to-all-start = ((bf16[2,128,4096]{1,0,2:T(2,128)(2,1)}), bf16[2,128,4096]{1,0,2:T(2,128)(2,1)}, u32[]{:S(2)}, u32[]{:S(2)}) async-start(bf16[2,128,4096]{1,0,2:T(2,128)(2,1)} %copy.145), calls=%async_computation | async-start | bytes 4194304 | tf_op jit(solution)/shard_map/all_to_all | solution.py:19
  111.8 1.6 copy-start.2
  152.5 1.6 copy-start
  153.4 28.8 %copy-start.3 = (f32[1,32,128,128]{2,3,1,0:T(8,128)}, f32[1,32,128,128]{2,3,1,0:T(8,128)S(1)}, u32[]{:S(2)}) copy-start(f32[1,32,128,128]{2,3,1,0:T(8,128)S(1)} %get-tuple-element.54) | copy-start | bytes 6291460
  155.7 1.6 copy-start.6
  245.4 120.9 %all-to-all-start.5 = ((bf16[32,2,8192]{2,1,0:T(2,128)(2,1)}), bf16[32,2,8192]{2,1,0:T(2,128)(2,1)}, u32[]{:S(2)}, u32[]{:S(2)}) async-start(bf16[32,2,8192]{2,1,0:T(2,128)(2,1)} %reshape.660), calls=%async_computation.5 | async-start | bytes 2097152 | tf_op jit(solution)/shard_map/all_to_all | solution.py:197
  268.7 3.7 copy-start.4
  268.7 3.7 copy-start.5
